TPU v7x, 32 devices: a whole 2x2x4 slice. The times are simulated.
32 devices in a mesh: fsdp: 4 (over y, x), tp: 8 (over z, core).
Axes of the slice: x: 2, y: 2, z: 4, core: 2. Of those that a mesh axis runs over, the one named last changes fastest.
Arguments:
- ref_gate: bfloat16 [3072, 11008], P('fsdp', 'tp'), may hold values from -6 to 6
- ref_up: bfloat16 [3072, 11008], P('fsdp', 'tp'), may hold values from -6 to 6
- ref_residual: bfloat16 [3072, 4096], P('fsdp', 'tp'), may hold values from -6 to 6
- ref_modality: int32 [3072], P('fsdp'), may hold values 0 or 1
- ref_down_text: bfloat16 [4096, 11008], P('fsdp', 'tp'), may hold values from -0.0546875 to 0.0546875
- ref_down_image: bfloat16 [4096, 11008], P('fsdp', 'tp'), may hold values from -0.0546875 to 0.0546875
- pol_gate: bfloat16 [3072, 11008], P('fsdp', 'tp'), may hold values from -6 to 6
- pol_up: bfloat16 [3072, 11008], P('fsdp', 'tp'), may hold values from -6 to 6
- pol_modality: int32 [3072], P('fsdp'), may hold values 0 or 1
- pol_segment: int32 [3072], P('fsdp'), may hold values from 0 to 5, never falling along the last dimension, each value on 1 to 768 neighbouring positions
- pair_margin: float32 [3], replicated, may hold values from -30 to 30
- token_cotangent: bfloat16 [3072, 4096], P('fsdp', 'tp'), may hold values from -24 to 24
- pol_down_text: bfloat16 [4096, 11008], P('fsdp', 'tp'), may hold values from -0.0546875 to 0.0546875
- pol_down_image: bfloat16 [4096, 11008], P('fsdp', 'tp'), may hold values from -0.0546875 to 0.0546875
Outputs:
- ref_out: bfloat16 [3072, 4096], P('fsdp', 'tp')
- grad_gate: bfloat16 [3072, 11008], P('fsdp', 'tp')
- grad_up: bfloat16 [3072, 11008], P('fsdp', 'tp')
- grad_down_text: float32 [4096, 11008], P('fsdp', 'tp')
- grad_down_image: float32 [4096, 11008], P('fsdp', 'tp')
Inputs may be any that keep to these rules, and one draw needn't show every extreme that they name: `ref_modality`: 0 marks a text token, 1 an image token. `pol_modality`: 0 marks a text token, 1 an image token. `pol_segment`: response numbers never fall along the tokens; responses 2p and 2p + 1 are the chosen and the rejected response of pair p; every response has at least one token.
All inputs are finite; a program needn't handle non-finite values. No bound on the sum of `ref_modality` or of `pol_modality` on one device may be relied on, other than what follows from the above.
Results may differ from a plain program's by a relative error of at most 0.015.
Values may be sent and summed in bfloat16 or wider, within the bound.
A program may use at most 192 MiB of HBM per device.

v0:
```python
import jax
import jax.numpy as jnp
from jax import lax
from jax.experimental import pallas as pl
from jax.experimental.pallas import tpu as pltpu
from jax.sharding import PartitionSpec as P


MESH = pl.DeviceIdType.MESH
LANES = 128
VMEM_BYTES = 67043328

dpo_beta = 0.1


def silu_parts(gate, up):
    gate_f = gate.astype(jnp.float32)
    up_f = up.astype(jnp.float32)
    sig = jax.nn.sigmoid(gate_f)
    act = gate_f * sig
    return gate_f, up_f, sig, act


def hidden_of(gate, up):
    _, up_f, _, act = silu_parts(gate, up)
    return (act * up_f).astype(jnp.bfloat16)


def coef_of(pol_segment, pair_margin):
    seg_ids = jnp.arange(2 * pair_margin.shape[0], dtype=jnp.int32)
    pair_weight = dpo_beta * jax.nn.sigmoid(-dpo_beta * pair_margin)
    table = jnp.repeat(pair_weight, 2) * jnp.where(seg_ids % 2 == 0, -1.0, 1.0).astype(jnp.float32)
    return jnp.sum(
        jnp.where(pol_segment[:, None] == seg_ids[None, :], table[None, :], jnp.float32(0.0)),
        axis=1,
    )


def swap_pairs(n_fsdp, n_tp):
    r = n_tp // n_fsdp
    return [
        (f * n_tp + q * r + j, q * n_tp + f * r + j)
        for f in range(n_fsdp)
        for q in range(n_fsdp)
        for j in range(r)
    ]


def gather_modality(ref_modality, pol_modality, n_fsdp):
    own = jnp.stack([ref_modality, pol_modality])
    me = lax.axis_index("fsdp")
    both = jnp.zeros((n_fsdp,) + own.shape, own.dtype)
    both = lax.dynamic_update_index_in_dim(both, own, me, 0)
    for s in range(1, n_fsdp):
        got = lax.ppermute(own, "fsdp", [(i, (i + s) % n_fsdp) for i in range(n_fsdp)])
        both = lax.dynamic_update_index_in_dim(both, got, (me - s) % n_fsdp, 0)
    return both[:, 0].reshape(-1), both[:, 1].reshape(-1)


def per_device(
    n_fsdp,
    n_tp,
    ref_gate,
    ref_up,
    ref_residual,
    ref_modality,
    ref_down_text,
    ref_down_image,
    pol_gate,
    pol_up,
    pol_modality,
    pol_segment,
    pair_margin,
    token_cotangent,
    pol_down_text,
    pol_down_image,
):
    rows, feats = token_cotangent.shape
    pairs = swap_pairs(n_fsdp, n_tp)
    partner = [(t, t ^ 1) for t in range(n_tp)]
    index = lax.axis_index("tp")
    line, half = index // 2, index % 2

    def shift(step):
        return [(t, (t + 2 * step) % n_tp) for t in range(n_tp)]

    coef = coef_of(pol_segment, pair_margin)
    pol_own = hidden_of(pol_gate, pol_up)
    pol_hidden = lax.all_gather(pol_own, "fsdp", axis=0, tiled=True)
    ref_own = hidden_of(ref_gate, ref_up)
    ref_hidden = lax.all_gather(ref_own, "fsdp", axis=0, tiled=True)

    local_cot = (coef[:, None] * token_cotangent.astype(jnp.float32)).astype(jnp.bfloat16)
    moved = lax.ppermute(local_cot, ("fsdp", "tp"), pairs)
    modality_r, modality_p = gather_modality(ref_modality, pol_modality, n_fsdp)
    image_r = (modality_r == 1)[:, None]
    image_p = (modality_p == 1)[:, None]

    mine = jnp.zeros((n_fsdp, rows, feats), jnp.bfloat16)
    mine = lax.dynamic_update_index_in_dim(mine, moved, line, 0)
    for s in range(1, n_fsdp):
        got = lax.ppermute(moved, "tp", shift(s))
        mine = lax.dynamic_update_index_in_dim(mine, got, (line - s) % n_fsdp, 0)
    mine = mine.reshape(n_fsdp * rows, feats)
    theirs = lax.ppermute(mine, "tp", partner)
    first = half == 0
    cot_full = jnp.concatenate(
        [jnp.where(first, mine, theirs), jnp.where(first, theirs, mine)], axis=1
    )

    dh_text = jnp.dot(cot_full, pol_down_text, preferred_element_type=jnp.float32)
    dh_image = jnp.dot(cot_full, pol_down_image, preferred_element_type=jnp.float32)
    dh_part = jnp.where(image_p, dh_image, dh_text).astype(jnp.bfloat16)
    d_hidden = lax.psum_scatter(dh_part, "fsdp", scatter_dimension=0, tiled=True)

    zero = jnp.zeros_like(cot_full)
    over_rows = (((0,), (0,)), ((), ()))
    g_text = lax.dot_general(
        jnp.where(image_p, zero, cot_full), pol_hidden, over_rows, preferred_element_type=jnp.float32
    )
    g_image = lax.dot_general(
        jnp.where(image_p, cot_full, zero), pol_hidden, over_rows, preferred_element_type=jnp.float32
    )

    contract = (((1,), (1,)), ((), ()))

    def out_half(which):
        w_text = lax.dynamic_slice_in_dim(ref_down_text, which * feats, feats, 0)
        w_image = lax.dynamic_slice_in_dim(ref_down_image, which * feats, feats, 0)
        o_text = lax.dot_general(ref_hidden, w_text, contract, preferred_element_type=jnp.float32)
        o_image = lax.dot_general(ref_hidden, w_image, contract, preferred_element_type=jnp.float32)
        return jnp.where(image_r, o_image, o_text).astype(jnp.bfloat16)

    got = lax.ppermute(out_half(1 - half), "tp", partner)
    keep = out_half(half)
    both = (keep.astype(jnp.float32) + got.astype(jnp.float32)).astype(jnp.bfloat16)
    both = both.reshape(n_fsdp, rows, feats)
    total = lax.dynamic_index_in_dim(both, line, 0, keepdims=False).astype(jnp.float32)
    for s in range(1, n_fsdp):
        piece = lax.dynamic_index_in_dim(both, (line + s) % n_fsdp, 0, keepdims=False)
        total = total + lax.ppermute(piece, "tp", shift(s)).astype(jnp.float32)
    summed = lax.ppermute(total.astype(jnp.bfloat16), ("fsdp", "tp"), pairs)
    ref_out = (summed.astype(jnp.float32) + ref_residual.astype(jnp.float32)).astype(jnp.bfloat16)

    late_gate, late_up, d_hidden = lax.optimization_barrier((pol_gate, pol_up, d_hidden))
    gate_f, up_f, sig, act = silu_parts(late_gate, late_up)
    d_hidden = d_hidden.astype(jnp.float32)
    grad_gate = (d_hidden * up_f * sig * (1.0 + gate_f * (1.0 - sig))).astype(jnp.bfloat16)
    grad_up = (d_hidden * act).astype(jnp.bfloat16)
    return (ref_out, grad_gate, grad_up, g_text, g_image)


def square_kernel(
    ref_gate, ref_up, mod_in, cot_in, ref_text, ref_image, pol_gate, pol_up, pol_text, pol_image,
    out_o, dh_own, dh_x, dh_y, hp_far, gt_o, gi_o, cot_far, mod_far,
    href, hpv, mod, abuf, cot, w, sis_send, sis_recv, zs, zr, fin, rb, dsend, drecv, gtile,
    ss, rs, ls, gs,
):
    n = cot.shape[1]
    rows, half = cot.shape[2], cot.shape[3]
    q = rows // n
    ff = href.shape[1]
    mid = ff // 2
    wide = 2 * LANES
    chunks = rows // wide
    f, t = lax.axis_index("fsdp"), lax.axis_index("tp")
    z, c = t // 2, t % 2
    oc = 1 - c
    fs = (f, f + 1 - 2 * (f % 2), (f + 2) % n, n - 1 - f)
    zp = [(z + r) % n for r in range(n)]
    zm = [(z + n - r) % n for r in range(n)]
    side = [(fs[s], t) for s in range(4)]
    up = [(f, 2 * zp[r] + c) for r in range(n)]
    sister = (f, 2 * z + oc)
    count = [0]
    lcount = [0]
    sends = []

    def remote(src, dst, dev):
        i = count[0]
        count[0] += 1
        copy = pltpu.make_async_remote_copy(
            src_ref=src, dst_ref=dst, send_sem=ss.at[i], recv_sem=rs.at[i],
            device_id=dev, device_id_type=MESH,
        )
        copy.start()
        sends.append(copy)
        return copy

    def local(src, dst):
        i = lcount[0]
        lcount[0] += 1
        copy = pltpu.make_async_copy(src, dst, ls.at[i])
        copy.start()
        return copy

    def piece(i):
        return pl.ds(pl.multiple_of(i * q, q), q)

    top, low = pl.ds(0, mid), pl.ds(mid, mid)
    loads = [
        [local(src.at[part], dsend.at[i, part]) for i, src in ((0, ref_gate), (1, ref_up))]
        for part in (top, low)
    ]
    a_own = local(cot_in.at[piece(z)], abuf.at[z])
    mod_own = local(mod_in, mod.at[0])
    w_ld = [local(ref_text, w.at[0]), local(ref_image, w.at[1])]
    pol_ld = [local(pol_gate, dsend.at[2]), local(pol_up, dsend.at[3])]

    barrier = pltpu.get_barrier_semaphore()
    peers = [side[1], side[2], side[3]] + [up[r] for r in range(1, n)] + [sister]
    for peer in peers:
        pl.semaphore_signal(barrier, inc=1, device_id=peer, device_id_type=MESH)
    pl.semaphore_wait(barrier, len(peers))

    a_cp = [remote(cot_in.at[piece(zp[r])], abuf.at[z], up[r]) for r in range(1, n)]
    m_cp = [remote(mod_in, mod.at[s], side[s]) for s in range(1, 4)]

    def hidden_rows(first, src, dst):
        @pl.loop(0, mid // 16)
        def _(i):
            at = pl.ds(pl.multiple_of(first + i * 16, 16), 16)
            gate = dsend[src, at, :].astype(jnp.float32)
            act = gate * jax.nn.sigmoid(gate)
            dst[0, at, :] = (act * dsend[src + 1, at, :].astype(jnp.float32)).astype(jnp.bfloat16)

    for copy in loads[0]:
        copy.wait()
    hidden_rows(0, 0, href)
    own_x = [remote(href.at[0, top], href.at[1, top], side[1])]
    for copy in loads[1]:
        copy.wait()
    hidden_rows(mid, 0, href)
    own_y = [remote(href.at[0, low], href.at[2, low], side[2])]
    for copy in pol_ld:
        copy.wait()
    hidden_rows(0, 2, hpv)
    hidden_rows(mid, 2, hpv)

    a_own.wait()
    for copy in a_cp:
        copy.wait_recv()
    b_cp = [remote(abuf.at[fs[s]], cot.at[c, s, piece(z)], side[s]) for s in range(1, 4)]
    own_x.append(remote(href.at[0, low], href.at[1, low], side[1]))
    own_y.append(remote(href.at[0, top], href.at[2, top], side[2]))
    cot[c, 0, piece(z), :] = abuf[f]

    def lanes(j, size):
        return pl.ds(pl.multiple_of(j * size, size), size)

    over_ff = (((0,), (0,)), ((), ()))

    def out_rows(s, j, which):
        cols = lanes(which, half)
        image = mod[s, :, lanes(j, wide)][0:1]
        h = href[s, :, lanes(j, wide)]
        h_image = h * image
        h_text = h * (1.0 - image)
        o_text = lax.dot_general(h_text, w[0, :, cols], over_ff, preferred_element_type=jnp.float32)
        o_image = lax.dot_general(h_image, w[1, :, cols], over_ff, preferred_element_type=jnp.float32)
        return o_text + o_image

    e_cp = {}
    f_cp = []

    def out_other(s):
        @pl.loop(0, chunks)
        def _(j):
            sis_send[s, lanes(j, wide), :] = out_rows(s, j, oc).astype(jnp.bfloat16)

        e_cp[s] = remote(sis_send.at[s], sis_recv.at[s], sister)

    def out_own(s):
        e_cp[s].wait_recv()

        @pl.loop(0, chunks)
        def _(j):
            total = out_rows(s, j, c) + sis_recv[s, lanes(j, wide), :].astype(jnp.float32)
            zs[s, lanes(j, wide), :] = total.astype(jnp.bfloat16)

        for r in range(1, n):
            f_cp.append(remote(zs.at[s, piece(zp[r])], zr.at[r - 1, s], up[r]))

    mod_own.wait()
    for copy in w_ld:
        copy.wait()
    out_other(0)
    for copy in b_cp:
        copy.wait_recv()
    c_cp = [remote(cot.at[c, :, piece(z)], cot.at[c, :, piece(z)], up[r]) for r in range(1, n)]
    d_cp = [remote(cot.at[c, :, piece(z)], cot.at[c, :, piece(z)], sister)]
    own_x[0].wait_recv()
    fwd_y = remote(href.at[1, top], href.at[3, top], side[2])
    own_y[0].wait_recv()
    fwd_x = remote(href.at[2, low], href.at[3, low], side[1])
    out_own(0)
    pol_x = [remote(hpv.at[0, part], hpv.at[1, part], side[1]) for part in (top, low)]
    pol_y = [remote(hpv.at[0, part], hpv.at[2, part], side[2]) for part in (low, top)]
    for copy in m_cp:
        copy.wait_recv()
    own_x[1].wait_recv()
    own_y[1].wait_recv()
    out_other(1)
    out_other(2)
    out_own(1)
    out_own(2)
    fwd_y.wait_recv()
    fwd_x.wait_recv()
    mod_cp = local(mod.at[3], mod_far)
    out_other(3)
    for r in range(1, n):
        c_cp[r - 1].wait_recv()
        d_cp.append(remote(cot.at[c, :, piece(zm[r])], cot.at[c, :, piece(zm[r])], sister))
    out_own(3)
    w_ld = [local(pol_text, w.at[0]), local(pol_image, w.at[1])]
    for copy in d_cp:
        copy.wait_recv()
    for copy in w_ld:
        copy.wait()
    far_cp = [local(cot.at[h, 3], cot_far.at[:, pl.ds(h * half, half)]) for h in range(2)]

    over_last = (((1,), (1,)), ((), ()))

    def dh_part(s, first, got):
        part = pl.ds(first, mid)

        @pl.loop(0, chunks)
        def _(j):
            at = lanes(j, wide)

            def of(i):
                lo = lax.dot_general(
                    w[i, part, :half], cot[0, s, at, :], over_last, preferred_element_type=jnp.float32
                )
                return lo + lax.dot_general(
                    w[i, part, half:], cot[1, s, at, :], over_last, preferred_element_type=jnp.float32
                )

            row = mod[s, :, at].astype(jnp.float32)[1:2]
            image = jnp.broadcast_to(row, (mid, wide)) > 0.5
            d = jnp.where(image, of(1), of(0))
            if got is not None:
                d = d + drecv[got, :, at].astype(jnp.float32)
            dsend[s, part, at] = d.astype(jnp.bfloat16)

    dh_part(3, 0, None)
    i_x = remote(dsend.at[3, top], drecv.at[0], side[1])
    dh_part(3, mid, None)
    i_y = remote(dsend.at[3, low], drecv.at[1], side[2])
    dh_part(1, 0, None)
    j_cp = [remote(dsend.at[1, top], dh_x.at[top], side[1])]
    dh_part(2, mid, None)
    j_cp.append(remote(dsend.at[2, low], dh_y.at[low], side[2]))
    for copy in pol_x + pol_y:
        copy.wait_recv()
    polf_y = remote(hpv.at[1, top], hp_far.at[top], side[2])
    polf_x = remote(hpv.at[2, low], hp_far.at[low], side[1])
    dh_part(0, 0, None)
    dh_part(0, mid, None)
    own_cp = local(dsend.at[0], dh_own)

    per_half = half // wide
    tiles = 2 * per_half

    def g_copies(i):
        slot, a, j = i % 2, i // tiles, i % tiles
        at = pl.ds(pl.multiple_of(a * mid, mid), mid)
        return (
            pltpu.make_async_copy(gtile.at[slot, 0], gt_o.at[at, lanes(j, wide)], gs.at[slot, 0]),
            pltpu.make_async_copy(gtile.at[slot, 1], gi_o.at[at, lanes(j, wide)], gs.at[slot, 1]),
        )

    @pl.loop(0, 2 * tiles)
    def _(i):
        a, j = i // tiles, i % tiles
        at = pl.ds(pl.multiple_of(a * mid, mid), mid)
        g_text, g_image = None, None
        for s in range(3):
            y = cot[j // per_half, s, :, lanes(j % per_half, wide)]
            image = mod[s][1:2]
            h = hpv[s, at, :]
            t_text = jnp.dot(h * (1.0 - image), y, preferred_element_type=jnp.float32)
            t_image = jnp.dot(h * image, y, preferred_element_type=jnp.float32)
            g_text = t_text if g_text is None else g_text + t_text
            g_image = t_image if g_image is None else g_image + t_image

        @pl.when(i >= 2)
        def _():
            for copy in g_copies(i - 2):
                copy.wait()

        gtile[i % 2, 0] = g_text
        gtile[i % 2, 1] = g_image
        for copy in g_copies(i):
            copy.start()

    i_y.wait_recv()
    dh_part(1, mid, 1)
    i_x.wait_recv()
    dh_part(2, 0, 0)

    for copy in f_cp:
        copy.wait_recv()
    for s in range(4):
        total = zs[s, piece(z), :].astype(jnp.float32)
        for r in range(1, n):
            total = total + zr[r - 1, s].astype(jnp.float32)
        fin[s] = total.astype(jnp.bfloat16)
    rb[f] = fin[0]
    g_cp = [remote(fin.at[s], rb.at[f], side[s]) for s in range(1, 4)]
    j_cp.append(remote(dsend.at[1, low], dh_x.at[low], side[1]))
    j_cp.append(remote(dsend.at[2, top], dh_y.at[top], side[2]))
    for copy in g_cp:
        copy.wait_recv()
    h_cp = [remote(rb.at[zp[r]], out_o.at[piece(z)], up[r]) for r in range(1, n)]
    h_own = local(rb.at[z], out_o.at[piece(z)])
    for i in (2 * tiles - 2, 2 * tiles - 1):
        for copy in g_copies(i):
            copy.wait()
    for copy in [h_own, own_cp, mod_cp] + far_cp:
        copy.wait()
    for copy in h_cp + [polf_x, polf_y] + j_cp:
        copy.wait_recv()
    for copy in sends:
        copy.wait_send()


def square_per_device(
    n_fsdp,
    n_tp,
    ref_gate,
    ref_up,
    ref_residual,
    ref_modality,
    ref_down_text,
    ref_down_image,
    pol_gate,
    pol_up,
    pol_modality,
    pol_segment,
    pair_margin,
    token_cotangent,
    pol_down_text,
    pol_down_image,
):
    rows, feats = token_cotangent.shape
    ff = ref_gate.shape[1]
    n = n_fsdp
    q = rows // n
    bf16 = jnp.bfloat16
    coef = coef_of(pol_segment, pair_margin)
    cot_in = (coef[:, None] * token_cotangent.astype(jnp.float32)).astype(bf16)
    row = lax.broadcasted_iota(jnp.int32, (16, rows), 0)
    mod_in = jnp.where(row == 0, ref_modality[None, :], jnp.where(row == 1, pol_modality[None, :], 0))
    mod_in = mod_in.astype(bf16)

    shape = jax.ShapeDtypeStruct
    block = shape((ff, rows), bf16)
    grad = shape((ff, 2 * feats), jnp.float32)
    anywhere = pl.BlockSpec(memory_space=pl.ANY)
    outs = (
        shape((rows, feats), bf16), block, block, block, block, grad, grad,
        shape((rows, 2 * feats), bf16), shape((16, rows), bf16),
    )
    scratch = [
        pltpu.VMEM((4, ff, rows), bf16),
        pltpu.VMEM((3, ff, rows), bf16),
        pltpu.VMEM((4, 16, rows), bf16),
        pltpu.VMEM((n, q, feats), bf16),
        pltpu.VMEM((2, 4, rows, feats), bf16),
        pltpu.VMEM((2, ff, 2 * feats), bf16),
        pltpu.VMEM((4, rows, feats), bf16),
        pltpu.VMEM((4, rows, feats), bf16),
        pltpu.VMEM((4, rows, feats), bf16),
        pltpu.VMEM((n - 1, 4, q, feats), bf16),
        pltpu.VMEM((4, q, feats), bf16),
        pltpu.VMEM((4, q, feats), bf16),
        pltpu.VMEM((4, ff, rows), bf16),
        pltpu.VMEM((2, ff // 2, rows), bf16),
        pltpu.VMEM((2, 2, ff // 2, 2 * LANES), jnp.float32),
        pltpu.SemaphoreType.DMA((64,)),
        pltpu.SemaphoreType.DMA((64,)),
        pltpu.SemaphoreType.DMA((24,)),
        pltpu.SemaphoreType.DMA((2, 2)),
    ]
    out, own, from_x, from_y, hp_far, g_text, g_image, cot_far, mod_far = pl.pallas_call(
        square_kernel,
        out_shape=outs,
        in_specs=[anywhere] * 10,
        out_specs=(anywhere,) * len(outs),
        scratch_shapes=scratch,
        compiler_params=pltpu.CompilerParams(
            collective_id=0, has_side_effects=True, vmem_limit_bytes=VMEM_BYTES
        ),
        name="square_step",
    )(
        ref_gate.T, ref_up.T, mod_in, cot_in, ref_down_text.T, ref_down_image.T,
        pol_gate.T, pol_up.T, pol_down_text.T, pol_down_image.T,
    )

    ref_out = (out.astype(jnp.float32) + ref_residual.astype(jnp.float32)).astype(bf16)

    gate_f, up_f, sig, act = silu_parts(pol_gate.T, pol_up.T)
    d_hidden = own.astype(jnp.float32) + from_x.astype(jnp.float32) + from_y.astype(jnp.float32)
    grad_gate = (d_hidden * up_f * sig * (1.0 + gate_f * (1.0 - sig))).astype(bf16)
    grad_up = (d_hidden * act).astype(bf16)

    image = mod_far[1:2] > 0.5
    zero = jnp.zeros_like(hp_far)
    g_text = g_text + jnp.dot(jnp.where(image, zero, hp_far), cot_far, preferred_element_type=jnp.float32)
    g_image = g_image + jnp.dot(jnp.where(image, hp_far, zero), cot_far, preferred_element_type=jnp.float32)
    return (ref_out, grad_gate.T, grad_up.T, g_text.T, g_image.T)


def solution(mesh):
    n_fsdp, n_tp = mesh.shape["fsdp"], mesh.shape["tp"]
    two = P("fsdp", "tp")
    one = P("fsdp")
    in_specs = (two, two, two, one, two, two, two, two, one, one, P(), two, two, two)
    square = n_fsdp == 4 and n_tp == 2 * n_fsdp
    plan = square_per_device if square else per_device

    def body(*args):
        return plan(n_fsdp, n_tp, *args)

    return jax.shard_map(
        body, mesh=mesh, in_specs=in_specs, out_specs=(two,) * 5, check_vma=False
    )
```

profile of v0, /device:TPU:28, one launch (start us, length us, event | category | flops | bytes accessed | tf_op | source)
XLA Modules:
  0.0 278.7 jit_solution(61491445687517006)
XLA Ops:
  0.6 1.4 select_convert_fusion.mod_in
  2.0 0.7 divide_multiply_fusion
  2.7 0.1 broadcast_in_dim.65
  2.8 0.1 reshape.33
  2.9 0.8 select_reduce_fusion
  3.6 2.2 multiply_convert_fusion.cot_in
  5.9 252.9 %square_step.1 = (bf16[768,512]{1,0:T(8,128)(2,1)}, bf16[1376,768]{1,0:T(8,128)(2,1)}, bf16[1376,768]{1,0:T(8,128)(2,1)}, bf16[1376,768]{1,0:T(8,128)(2,1)}, bf1...) custom-call(bf16[1376,768]{1,0:T(8,128)(2,1)} %bitcast.27, ...), custom_call_target="tpu_custom_call" | custom-call | tf_op jit(solution)/shard_map/square_step/pallas_call | solution.py:486
  258.8 0.0 copy-start
  258.8 0.0 slice-start.2
  258.8 2.6 add_convert_fusion
  261.4 0.0 copy-done
  261.4 0.0 slice-start.3
  261.4 0.0 copy-start.1
  261.4 0.0 copy-start.2
  261.5 0.0 slice-start
  261.5 6.4 %fusion.12 = (bf16[768,1376]{0,1:T(8,128)(2,1)}, bf16[768,1376]{0,1:T(8,128)(2,1)}) fusion(bf16[1376,768]{1,0:T(8,128)(2,1)} %get-tuple-element.17, bf16[1376,768]{1,0:T(8,128)(2,1)} %get-tuple-element.16, bf16[1376,768]{1,0:T(8,128)(2,1)} %get-tuple-element.15, bf16[768,1376]{0,1:T(8,128)(2,1)S(1)} %copy-done, bf16[768,1376]{0,1:T(8,128)(2,1)} %param.21), kind=kLoop, calls=%fused_computation.18 | loop fusion | flops 21135360 | bytes 14794752 | tf_op jit(solution)/shard_map/transpose | solution.py:512
  267.9 0.7 compare_reduce_fusion
  268.6 0.0 slice-done.2
  268.6 0.0 slice-done.3
  268.6 0.0 copy-done.1
  268.6 0.0 copy-done.2
  268.7 0.0 slice-start.1
  268.7 5.0 %add_bitcast_fusion.1 = f32[1024,1376]{0,1:T(8,128)} fusion(f32[1376,1024]{1,0:T(8,128)S(1)} %bitcast.32, bf16[768,1024]{1,0:T(8,128)(2,1)S(1)} %copy-done.2, bf16[1376,768]{1,0:T(8,128)(2,1)S(1)} %copy-done.1, pred[768]{0:T(1024)(128)(4,1)S(1)} %compare_reduce_fusion), kind=kOutput, calls=%fused_computation.4 | convolution fusion | flops 2166726656 | bytes 14959360 | tf_op jit(solution)/shard_map/dot_general | solution.py:510
  273.7 0.0 slice-done
  273.7 0.0 slice-done.1
  273.7 5.0 %add_bitcast_fusion = f32[1024,1376]{0,1:T(8,128)} fusion(f32[1376,1024]{1,0:T(8,128)S(1)} %bitcast.30, bf16[768,1024]{1,0:T(8,128)(2,1)S(1)} %copy-done.2, bf16[1376,768]{1,0:T(8,128)(2,1)S(1)} %copy-done.1, pred[768]{0:T(1024)(128)(4,1)S(1)} %compare_reduce_fusion), kind=kOutput, calls=%fused_computation.3 | convolution fusion | flops 2166726656 | bytes 14959360 | tf_op jit(solution)/shard_map/dot_general | solution.py:511
  (4 shorter events, 0.0 us)
Async XLA Ops:
  258.8 2.6 copy-start
  258.8 9.8 %slice-start.2 = ((s8[5636096]{0:T(1024)(128)(4,1)}), s8[4194304]{0:T(1024)(128)(4,1)S(1)}, s32[]{:S(2)}) async-start(s8[5636096]{0:T(1024)(128)(4,1)} %bitcast.31), calls=%async_computation.2 | async-start | bytes 8388608
  261.4 7.2 %slice-start.3 = ((s8[5636096]{0:T(1024)(128)(4,1)}), s8[1441792]{0:T(1024)(128)(4,1)S(1)}, s32[]{:S(2)}) async-start(s8[5636096]{0:T(1024)(128)(4,1)} %bitcast.31), calls=%async_computation.3 | async-start | bytes 2883584
  261.4 7.2 %copy-start.1 = (bf16[1376,768]{1,0:T(8,128)(2,1)S(1)}, bf16[1376,768]{1,0:T(8,128)(2,1)}, u32[]{:S(2)}) copy-start(bf16[1376,768]{1,0:T(8,128)(2,1)} %get-tuple-element.20) | copy-start | bytes 6340612
  261.4 7.2 %copy-start.2 = (bf16[768,1024]{1,0:T(8,128)(2,1)S(1)}, bf16[768,1024]{1,0:T(8,128)(2,1)}, u32[]{:S(2)}) copy-start(bf16[768,1024]{1,0:T(8,128)(2,1)} %get-tuple-element.21) | copy-start | bytes 4718596
  261.5 12.2 %slice-start = ((s8[5636096]{0:T(1024)(128)(4,1)}), s8[1441792]{0:T(1024)(128)(4,1)S(1)}, s32[]{:S(2)}) async-start(s8[5636096]{0:T(1024)(128)(4,1)} %bitcast.29), calls=%async_computation | async-start | bytes 2883584
  268.7 5.0 %slice-start.1 = ((s8[5636096]{0:T(1024)(128)(4,1)}), s8[4194304]{0:T(1024)(128)(4,1)S(1)}, s32[]{:S(2)}) async-start(s8[5636096]{0:T(1024)(128)(4,1)} %bitcast.29), calls=%async_computation.1 | async-start | bytes 8388608
where the time goes:
time: 279 us
  Pallas kernels  253 us (91%)
  other arithmetic  14.9 us (5%)
  matrix products  10 us (4%)
    pallas_call x1, Pallas kernels, square_per_device(): pl.pallas_call(square_kernel, out_shape=outs, in_specs=[anywhere] * 10, o...  253 us
    transpose x1, other arithmetic, square_per_device(): return (ref_out, grad_gate.T, grad_up.T, g_text.T, g_image.T)  6.43 us

commit v1 on v0

--- a/solution.py
+++ b/solution.py
@@ -151,9 +151,10 @@
 
 
 def square_kernel(
-    ref_gate, ref_up, mod_in, cot_in, ref_text, ref_image, pol_gate, pol_up, pol_text, pol_image,
-    out_o, dh_own, dh_x, dh_y, hp_far, gt_o, gi_o, cot_far, mod_far,
-    href, hpv, mod, abuf, cot, w, sis_send, sis_recv, zs, zr, fin, rb, dsend, drecv, gtile,
+    margin, ref_gate, ref_up, residual, ref_mod, ref_text, ref_image, pol_gate, pol_up, pol_mod, pol_seg, cot_raw,
+    pol_text, pol_image,
+    out_o, gg_o, gu_o, gt_o, gi_o,
+    href, hpv, tags, mod, own_cot, abuf, cot, w, sis_send, sis_recv, zs, zr, fin, rb, ra, dsend, drecv, dxy, gtile,
     ss, rs, ls, gs,
 ):
     n = cot.shape[1]
@@ -202,8 +203,8 @@
         [local(src.at[part], dsend.at[i, part]) for i, src in ((0, ref_gate), (1, ref_up))]
         for part in (top, low)
     ]
-    a_own = local(cot_in.at[piece(z)], abuf.at[z])
-    mod_own = local(mod_in, mod.at[0])
+    small = [local(src, tags.at[i]) for i, src in enumerate((ref_mod, pol_mod, pol_seg))]
+    small.append(local(cot_raw, own_cot))
     w_ld = [local(ref_text, w.at[0]), local(ref_image, w.at[1])]
     pol_ld = [local(pol_gate, dsend.at[2]), local(pol_up, dsend.at[3])]
 
@@ -212,9 +213,6 @@
     for peer in peers:
         pl.semaphore_signal(barrier, inc=1, device_id=peer, device_id_type=MESH)
     pl.semaphore_wait(barrier, len(peers))
-
-    a_cp = [remote(cot_in.at[piece(zp[r])], abuf.at[z], up[r]) for r in range(1, n)]
-    m_cp = [remote(mod_in, mod.at[s], side[s]) for s in range(1, 4)]
 
     def hidden_rows(first, src, dst):
         @pl.loop(0, mid // 16)
@@ -232,12 +230,32 @@
         copy.wait()
     hidden_rows(mid, 0, href)
     own_y = [remote(href.at[0, low], href.at[2, low], side[2])]
+    for copy in small:
+        copy.wait()
+
+    def tag_row(i, size):
+        return jnp.concatenate(
+            [jnp.broadcast_to(tags[i, j : j + 1, :], (size, LANES)) for j in range(rows // LANES)], axis=1
+        )
+
+    seg = tag_row(2, 8)
+    coef = jnp.zeros((8, rows), jnp.float32)
+    for p in range(margin.shape[0]):
+        weight = dpo_beta * jax.nn.sigmoid(-dpo_beta * jnp.full((8, rows), margin[p], jnp.float32))
+        coef = jnp.where(seg // 2 == p, weight, coef)
+    coef = jnp.where(seg % 2 == 0, -coef, coef).T[:, 0:1]
+    own_cot[...] = (coef * own_cot[...].astype(jnp.float32)).astype(jnp.bfloat16)
+    row = lax.broadcasted_iota(jnp.int32, (16, rows), 0)
+    both = jnp.where(row == 0, tag_row(0, 16), jnp.where(row == 1, tag_row(1, 16), 0))
+    mod[0] = both.astype(jnp.float32).astype(jnp.bfloat16)
+    a_cp = [remote(own_cot.at[piece(zp[r])], abuf.at[z], up[r]) for r in range(1, n)]
+    m_cp = [remote(mod.at[0], mod.at[s], side[s]) for s in range(1, 4)]
+    abuf[z] = own_cot[piece(z), :]
     for copy in pol_ld:
         copy.wait()
     hidden_rows(0, 2, hpv)
     hidden_rows(mid, 2, hpv)
 
-    a_own.wait()
     for copy in a_cp:
         copy.wait_recv()
     b_cp = [remote(abuf.at[fs[s]], cot.at[c, s, piece(z)], side[s]) for s in range(1, 4)]
@@ -281,7 +299,6 @@
         for r in range(1, n):
             f_cp.append(remote(zs.at[s, piece(zp[r])], zr.at[r - 1, s], up[r]))
 
-    mod_own.wait()
     for copy in w_ld:
         copy.wait()
     out_other(0)
@@ -306,18 +323,24 @@
     out_own(2)
     fwd_y.wait_recv()
     fwd_x.wait_recv()
-    mod_cp = local(mod.at[3], mod_far)
     out_other(3)
+    out_own(3)
+    pol_x[0].wait_recv()
+    polf_y = remote(hpv.at[1, top], hpv.at[3, top], side[2])
+    pol_y[0].wait_recv()
+    polf_x = remote(hpv.at[2, low], hpv.at[3, low], side[1])
     for r in range(1, n):
         c_cp[r - 1].wait_recv()
         d_cp.append(remote(cot.at[c, :, piece(zm[r])], cot.at[c, :, piece(zm[r])], sister))
-    out_own(3)
     w_ld = [local(pol_text, w.at[0]), local(pol_image, w.at[1])]
     for copy in d_cp:
         copy.wait_recv()
     for copy in w_ld:
         copy.wait()
-    far_cp = [local(cot.at[h, 3], cot_far.at[:, pl.ds(h * half, half)]) for h in range(2)]
+    waited = own_x + own_y + [fwd_x, fwd_y] + a_cp
+    for copy in waited:
+        copy.wait_send()
+    gate_ld = [local(pol_gate, href.at[0]), local(pol_up, href.at[1]), local(residual, own_cot)]
 
     over_last = (((1,), (1,)), ((), ()))
 
@@ -348,17 +371,30 @@
     dh_part(3, mid, None)
     i_y = remote(dsend.at[3, low], drecv.at[1], side[2])
     dh_part(1, 0, None)
-    j_cp = [remote(dsend.at[1, top], dh_x.at[top], side[1])]
+    j_cp = [remote(dsend.at[1, top], dxy.at[0, top], side[1])]
     dh_part(2, mid, None)
-    j_cp.append(remote(dsend.at[2, low], dh_y.at[low], side[2]))
-    for copy in pol_x + pol_y:
-        copy.wait_recv()
-    polf_y = remote(hpv.at[1, top], hp_far.at[top], side[2])
-    polf_x = remote(hpv.at[2, low], hp_far.at[low], side[1])
+    j_cp.append(remote(dsend.at[2, low], dxy.at[1, low], side[2]))
     dh_part(0, 0, None)
     dh_part(0, mid, None)
-    own_cp = local(dsend.at[0], dh_own)
-
+
+    for copy in f_cp:
+        copy.wait_recv()
+    for s in range(4):
+        total = zs[s, piece(z), :].astype(jnp.float32)
+        for r in range(1, n):
+            total = total + zr[r - 1, s].astype(jnp.float32)
+        fin[s] = total.astype(jnp.bfloat16)
+    rb[f] = fin[0]
+    g_cp = [remote(fin.at[s], rb.at[f], side[s]) for s in range(1, 4)]
+    i_y.wait_recv()
+    dh_part(1, mid, 1)
+    j_cp.append(remote(dsend.at[1, low], dxy.at[0, low], side[1]))
+    i_x.wait_recv()
+    dh_part(2, 0, 0)
+    j_cp.append(remote(dsend.at[2, top], dxy.at[1, top], side[2]))
+
+    for copy in [pol_x[1], pol_y[1], polf_x, polf_y]:
+        copy.wait_recv()
     per_half = half // wide
     tiles = 2 * per_half
 
@@ -375,7 +411,7 @@
         a, j = i // tiles, i % tiles
         at = pl.ds(pl.multiple_of(a * mid, mid), mid)
         g_text, g_image = None, None
-        for s in range(3):
+        for s in range(4):
             y = cot[j // per_half, s, :, lanes(j % per_half, wide)]
             image = mod[s][1:2]
             h = hpv[s, at, :]
@@ -394,35 +430,42 @@
         for copy in g_copies(i):
             copy.start()
 
-    i_y.wait_recv()
-    dh_part(1, mid, 1)
-    i_x.wait_recv()
-    dh_part(2, 0, 0)
-
-    for copy in f_cp:
-        copy.wait_recv()
-    for s in range(4):
-        total = zs[s, piece(z), :].astype(jnp.float32)
-        for r in range(1, n):
-            total = total + zr[r - 1, s].astype(jnp.float32)
-        fin[s] = total.astype(jnp.bfloat16)
-    rb[f] = fin[0]
-    g_cp = [remote(fin.at[s], rb.at[f], side[s]) for s in range(1, 4)]
-    j_cp.append(remote(dsend.at[1, low], dh_x.at[low], side[1]))
-    j_cp.append(remote(dsend.at[2, top], dh_y.at[top], side[2]))
     for copy in g_cp:
         copy.wait_recv()
-    h_cp = [remote(rb.at[zp[r]], out_o.at[piece(z)], up[r]) for r in range(1, n)]
-    h_own = local(rb.at[z], out_o.at[piece(z)])
+    h_cp = [remote(rb.at[zp[r]], ra.at[z], up[r]) for r in range(1, n)]
+    ra[z] = rb[z]
     for i in (2 * tiles - 2, 2 * tiles - 1):
         for copy in g_copies(i):
             copy.wait()
-    for copy in [h_own, own_cp, mod_cp] + far_cp:
-        copy.wait()
-    for copy in h_cp + [polf_x, polf_y] + j_cp:
-        copy.wait_recv()
+    for copy in gate_ld:
+        copy.wait()
+    for copy in h_cp:
+        copy.wait_recv()
+    total = own_cot[...].astype(jnp.float32) + ra[...].reshape(rows, half).astype(jnp.float32)
+    own_cot[...] = total.astype(jnp.bfloat16)
+    done = [local(own_cot, out_o)]
+
+    def grad_rows(first):
+        @pl.loop(0, mid // 16)
+        def _(i):
+            at = pl.ds(pl.multiple_of(first + i * 16, 16), 16)
+            d = dsend[0, at, :].astype(jnp.float32)
+            d = d + dxy[0, at, :].astype(jnp.float32) + dxy[1, at, :].astype(jnp.float32)
+            gate, up_f = href[0, at, :].astype(jnp.float32), href[1, at, :].astype(jnp.float32)
+            sig = jax.nn.sigmoid(gate)
+            href[2, at, :] = (d * up_f * sig * (1.0 + gate * (1.0 - sig))).astype(jnp.bfloat16)
+            href[3, at, :] = (d * gate * sig).astype(jnp.bfloat16)
+
+    for first, part, pair in ((0, top, (0, 3)), (mid, low, (1, 2))):
+        for i in pair:
+            j_cp[i].wait_recv()
+        grad_rows(first)
+        done += [local(href.at[2, part], gg_o.at[part]), local(href.at[3, part], gu_o.at[part])]
     for copy in sends:
-        copy.wait_send()
+        if all(copy is not other for other in waited):
+            copy.wait_send()
+    for copy in done:
+        copy.wait()
 
 
 def square_per_device(
@@ -448,24 +491,17 @@
     n = n_fsdp
     q = rows // n
     bf16 = jnp.bfloat16
-    coef = coef_of(pol_segment, pair_margin)
-    cot_in = (coef[:, None] * token_cotangent.astype(jnp.float32)).astype(bf16)
-    row = lax.broadcasted_iota(jnp.int32, (16, rows), 0)
-    mod_in = jnp.where(row == 0, ref_modality[None, :], jnp.where(row == 1, pol_modality[None, :], 0))
-    mod_in = mod_in.astype(bf16)
-
     shape = jax.ShapeDtypeStruct
     block = shape((ff, rows), bf16)
     grad = shape((ff, 2 * feats), jnp.float32)
     anywhere = pl.BlockSpec(memory_space=pl.ANY)
-    outs = (
-        shape((rows, feats), bf16), block, block, block, block, grad, grad,
-        shape((rows, 2 * feats), bf16), shape((16, rows), bf16),
-    )
+    outs = (shape((rows, feats), bf16), block, block, grad, grad)
     scratch = [
         pltpu.VMEM((4, ff, rows), bf16),
-        pltpu.VMEM((3, ff, rows), bf16),
+        pltpu.VMEM((4, ff, rows), bf16),
+        pltpu.VMEM((3, rows // LANES, LANES), jnp.int32),
         pltpu.VMEM((4, 16, rows), bf16),
+        pltpu.VMEM((rows, feats), bf16),
         pltpu.VMEM((n, q, feats), bf16),
         pltpu.VMEM((2, 4, rows, feats), bf16),
         pltpu.VMEM((2, ff, 2 * feats), bf16),
@@ -475,18 +511,20 @@
         pltpu.VMEM((n - 1, 4, q, feats), bf16),
         pltpu.VMEM((4, q, feats), bf16),
         pltpu.VMEM((4, q, feats), bf16),
+        pltpu.VMEM((4, q, feats), bf16),
         pltpu.VMEM((4, ff, rows), bf16),
         pltpu.VMEM((2, ff // 2, rows), bf16),
+        pltpu.VMEM((2, ff, rows), bf16),
         pltpu.VMEM((2, 2, ff // 2, 2 * LANES), jnp.float32),
         pltpu.SemaphoreType.DMA((64,)),
         pltpu.SemaphoreType.DMA((64,)),
-        pltpu.SemaphoreType.DMA((24,)),
+        pltpu.SemaphoreType.DMA((32,)),
         pltpu.SemaphoreType.DMA((2, 2)),
     ]
-    out, own, from_x, from_y, hp_far, g_text, g_image, cot_far, mod_far = pl.pallas_call(
+    ref_out, grad_gate, grad_up, g_text, g_image = pl.pallas_call(
         square_kernel,
         out_shape=outs,
-        in_specs=[anywhere] * 10,
+        in_specs=[pl.BlockSpec(memory_space=pltpu.SMEM)] + [anywhere] * 13,
         out_specs=(anywhere,) * len(outs),
         scratch_shapes=scratch,
         compiler_params=pltpu.CompilerParams(
@@ -494,21 +532,10 @@
         ),
         name="square_step",
     )(
-        ref_gate.T, ref_up.T, mod_in, cot_in, ref_down_text.T, ref_down_image.T,
-        pol_gate.T, pol_up.T, pol_down_text.T, pol_down_image.T,
+        pair_margin, ref_gate.T, ref_up.T, ref_residual, ref_modality.reshape(-1, LANES), ref_down_text.T, ref_down_image.T,
+        pol_gate.T, pol_up.T, pol_modality.reshape(-1, LANES), pol_segment.reshape(-1, LANES), token_cotangent,
+        pol_down_text.T, pol_down_image.T,
     )
-
-    ref_out = (out.astype(jnp.float32) + ref_residual.astype(jnp.float32)).astype(bf16)
-
-    gate_f, up_f, sig, act = silu_parts(pol_gate.T, pol_up.T)
-    d_hidden = own.astype(jnp.float32) + from_x.astype(jnp.float32) + from_y.astype(jnp.float32)
-    grad_gate = (d_hidden * up_f * sig * (1.0 + gate_f * (1.0 - sig))).astype(bf16)
-    grad_up = (d_hidden * act).astype(bf16)
-
-    image = mod_far[1:2] > 0.5
-    zero = jnp.zeros_like(hp_far)
-    g_text = g_text + jnp.dot(jnp.where(image, zero, hp_far), cot_far, preferred_element_type=jnp.float32)
-    g_image = g_image + jnp.dot(jnp.where(image, hp_far, zero), cot_far, preferred_element_type=jnp.float32)
     return (ref_out, grad_gate.T, grad_up.T, g_text.T, g_image.T)
 
 

time: 279 us -> 251 us (0.90)
  Pallas kernels: 253 us -> 236 us
  other arithmetic: 14.9 us -> 0.01 us
  local copies, waits for them, and re-layouts: 0.19 us -> 13.3 us
  matrix products: 10 us -> 0 us
    pallas_call x1, Pallas kernels: 253 us -> 236 us  [square_per_device(): pl.pallas_call(square_kernel, out_shape=outs, in_specs=[pl.BlockSpec(memo...]
    unnamed x14 -> x13, local copies, waits for them, and re-layouts: 0.03 us -> 13.3 us
    dot_general x2 -> x0, matrix products: 10 us -> none  [the longest x1 5.02 us: square_per_device(): jnp.dot(jnp.where(image, zero, hp_far), cot_far, preferred_element_type=j...]
    transpose x1 -> x0, other arithmetic: 6.43 us -> none  [square_per_device(): return (ref_out, grad_gate.T, grad_up.T, g_text.T, g_image.T)]
    convert_element_type x3 -> x0, other arithmetic: 6.25 us -> none  [the longest x1 2.61 us: square_per_device(): (out.astype(jnp.float32) + ref_residual.astype(jnp.float32)).astype(bf16)]
where the time goes in v1:
time: 251 us; the launch traced here: 250 us
  Pallas kernels  236 us (94%)
  local copies, waits for them, and re-layouts  13.3 us (5%)
    pallas_call x1, Pallas kernels, square_per_device(): pl.pallas_call(square_kernel, out_shape=outs, in_specs=[pl.BlockSpec(memo...  236 us
    unnamed x13, local copies, waits for them, and re-layouts  13.3 us

profile of v1, /device:TPU:28, one launch (start us, length us, event | category | flops | bytes accessed | tf_op | source)
XLA Modules:
  0.0 250.0 jit_solution(17624828215482336258)
XLA Ops:
  0.6 236.0 %square_step.1 = (bf16[768,512]{1,0:T(8,128)(2,1)}, bf16[1376,768]{1,0:T(8,128)(2,1)}, bf16[1376,768]{1,0:T(8,128)(2,1)}, f32[1376,1024]{1,0:T(8,128)}, f32[1376,1024]{1,0:T(8,128)}) custom-call(f32[3]{0:T(128)} %margin.1, bf16[1376,768]{1,0:T(8,128)(2,1)} %bitcast.23, bf16[1376,768]{1,0:T(8,128)(2,1)} %bitcast.24, bf16[768,512]{1,0:T(8,128)(2,1)} %residual.1, ...), custom_call_target="tpu_custom_call" | custom-call | tf_op jit(solution)/shard_map/square_step/pallas_call | solution.py:524
  236.7 0.0 copy-start.1
  236.7 2.2 copy.24
  238.9 0.0 copy-start
  238.9 3.2 %copy.25 = bf16[768,1376]{0,1:T(8,128)(2,1)} copy(bf16[768,1376]{0,1:T(8,128)(2,1)} %bitcast.28) | data formatting | bytes 4227072
  242.1 0.0 copy-done.1
  242.1 0.0 slice-start
  242.1 1.3 copy.26
  243.4 0.0 copy-done
  243.4 0.0 slice-start.1
  243.4 2.9 %copy.27 = f32[1024,1376]{0,1:T(8,128)} copy(f32[1024,1376]{0,1:T(8,128)S(1)} %bitcast.18) | data formatting | bytes 11272192
  246.3 0.5 slice-done
  246.8 0.8 slice-done.1
  247.5 2.5 copy.28
  (1 shorter events, 0.0 us)
Async XLA Ops:
  236.7 5.4 %copy-start.1 = (bf16[1376,768]{1,0:T(8,128)(2,1)S(1)}, bf16[1376,768]{1,0:T(8,128)(2,1)}, u32[]{:S(2)}) copy-start(bf16[1376,768]{1,0:T(8,128)(2,1)} %get-tuple-element.12) | copy-start | bytes 6340612
  238.9 4.5 %copy-start = (f32[1376,1024]{1,0:T(8,128)S(1)}, f32[1376,1024]{1,0:T(8,128)}, u32[]{:S(2)}) copy-start(f32[1376,1024]{1,0:T(8,128)} %get-tuple-element.13) | copy-start | bytes 16908292
  242.1 4.7 %slice-start = ((s8[5636096]{0:T(1024)(128)(4,1)}), s8[4194304]{0:T(1024)(128)(4,1)S(1)}, s32[]{:S(2)}) async-start(s8[5636096]{0:T(1024)(128)(4,1)} %bitcast.15), calls=%async_computation | async-start | bytes 8388608
  243.4 4.1 %slice-start.1 = ((s8[5636096]{0:T(1024)(128)(4,1)}), s8[1441792]{0:T(1024)(128)(4,1)S(1)}, s32[]{:S(2)}) async-start(s8[5636096]{0:T(1024)(128)(4,1)} %bitcast.15), calls=%async_computation.1 | async-start | bytes 2883584

commit v2 on v1

--- a/solution.py
+++ b/solution.py
@@ -153,8 +153,8 @@
 def square_kernel(
     margin, ref_gate, ref_up, residual, ref_mod, ref_text, ref_image, pol_gate, pol_up, pol_mod, pol_seg, cot_raw,
     pol_text, pol_image,
-    out_o, gg_o, gu_o, gt_o, gi_o,
-    href, hpv, tags, mod, own_cot, abuf, cot, w, sis_send, sis_recv, zs, zr, fin, rb, ra, dsend, drecv, dxy, gtile,
+    out_o, own_o, got_o, early_x, late_x, early_y, late_y, gt_o, gi_o,
+    href, hpv, tags, mod, own_cot, abuf, cot, w, sis_send, sis_recv, zs, zr, fin, rb, ra, dsend, drecv, gtile,
     ss, rs, ls, gs,
 ):
     n = cot.shape[1]
@@ -337,10 +337,9 @@
         copy.wait_recv()
     for copy in w_ld:
         copy.wait()
-    waited = own_x + own_y + [fwd_x, fwd_y] + a_cp
-    for copy in waited:
+    for copy in a_cp:
         copy.wait_send()
-    gate_ld = [local(pol_gate, href.at[0]), local(pol_up, href.at[1]), local(residual, own_cot)]
+    res_ld = local(residual, own_cot)
 
     over_last = (((1,), (1,)), ((), ()))
 
@@ -371,27 +370,10 @@
     dh_part(3, mid, None)
     i_y = remote(dsend.at[3, low], drecv.at[1], side[2])
     dh_part(1, 0, None)
-    j_cp = [remote(dsend.at[1, top], dxy.at[0, top], side[1])]
     dh_part(2, mid, None)
-    j_cp.append(remote(dsend.at[2, low], dxy.at[1, low], side[2]))
     dh_part(0, 0, None)
     dh_part(0, mid, None)
-
-    for copy in f_cp:
-        copy.wait_recv()
-    for s in range(4):
-        total = zs[s, piece(z), :].astype(jnp.float32)
-        for r in range(1, n):
-            total = total + zr[r - 1, s].astype(jnp.float32)
-        fin[s] = total.astype(jnp.bfloat16)
-    rb[f] = fin[0]
-    g_cp = [remote(fin.at[s], rb.at[f], side[s]) for s in range(1, 4)]
-    i_y.wait_recv()
-    dh_part(1, mid, 1)
-    j_cp.append(remote(dsend.at[1, low], dxy.at[0, low], side[1]))
-    i_x.wait_recv()
-    dh_part(2, 0, 0)
-    j_cp.append(remote(dsend.at[2, top], dxy.at[1, top], side[2]))
+    done = [local(dsend.at[0], own_o)]
 
     for copy in [pol_x[1], pol_y[1], polf_x, polf_y]:
         copy.wait_recv()
@@ -406,8 +388,7 @@
             pltpu.make_async_copy(gtile.at[slot, 1], gi_o.at[at, lanes(j, wide)], gs.at[slot, 1]),
         )
 
-    @pl.loop(0, 2 * tiles)
-    def _(i):
+    def g_tile(i):
         a, j = i // tiles, i % tiles
         at = pl.ds(pl.multiple_of(a * mid, mid), mid)
         g_text, g_image = None, None
@@ -430,42 +411,108 @@
         for copy in g_copies(i):
             copy.start()
 
+    pl.loop(0, tiles)(g_tile)
+
+    for copy in f_cp:
+        copy.wait_recv()
+    for s in range(4):
+        total = zs[s, piece(z), :].astype(jnp.float32)
+        for r in range(1, n):
+            total = total + zr[r - 1, s].astype(jnp.float32)
+        fin[s] = total.astype(jnp.bfloat16)
+    rb[f] = fin[0]
+    g_cp = [remote(fin.at[s], rb.at[f], side[s]) for s in range(1, 4)]
+    j_cp = [
+        remote(dsend.at[1, top], got_o.at[top], side[1]),
+        remote(dsend.at[2, low], got_o.at[low], side[2]),
+    ]
+    i_y.wait_recv()
+    dh_part(1, mid, 1)
+    fore, aft = pl.ds(0, early_x.shape[1]), pl.ds(early_x.shape[1], late_x.shape[1])
+    done += [local(dsend.at[1, low, fore], early_x), local(dsend.at[1, low, aft], late_x)]
+    i_x.wait_recv()
+    dh_part(2, 0, 0)
+    done += [local(dsend.at[2, top, fore], early_y), local(dsend.at[2, top, aft], late_y)]
     for copy in g_cp:
         copy.wait_recv()
     h_cp = [remote(rb.at[zp[r]], ra.at[z], up[r]) for r in range(1, n)]
     ra[z] = rb[z]
+    pl.loop(tiles, 2 * tiles)(g_tile)
+    res_ld.wait()
+    for copy in h_cp:
+        copy.wait_recv()
+    total = own_cot[...].astype(jnp.float32) + ra[...].reshape(rows, half).astype(jnp.float32)
+    own_cot[...] = total.astype(jnp.bfloat16)
+    done.append(local(own_cot, out_o))
     for i in (2 * tiles - 2, 2 * tiles - 1):
         for copy in g_copies(i):
             copy.wait()
-    for copy in gate_ld:
-        copy.wait()
-    for copy in h_cp:
-        copy.wait_recv()
-    total = own_cot[...].astype(jnp.float32) + ra[...].reshape(rows, half).astype(jnp.float32)
-    own_cot[...] = total.astype(jnp.bfloat16)
-    done = [local(own_cot, out_o)]
-
-    def grad_rows(first):
-        @pl.loop(0, mid // 16)
-        def _(i):
-            at = pl.ds(pl.multiple_of(first + i * 16, 16), 16)
-            d = dsend[0, at, :].astype(jnp.float32)
-            d = d + dxy[0, at, :].astype(jnp.float32) + dxy[1, at, :].astype(jnp.float32)
-            gate, up_f = href[0, at, :].astype(jnp.float32), href[1, at, :].astype(jnp.float32)
-            sig = jax.nn.sigmoid(gate)
-            href[2, at, :] = (d * up_f * sig * (1.0 + gate * (1.0 - sig))).astype(jnp.bfloat16)
-            href[3, at, :] = (d * gate * sig).astype(jnp.bfloat16)
-
-    for first, part, pair in ((0, top, (0, 3)), (mid, low, (1, 2))):
-        for i in pair:
-            j_cp[i].wait_recv()
-        grad_rows(first)
-        done += [local(href.at[2, part], gg_o.at[part]), local(href.at[3, part], gu_o.at[part])]
-    for copy in sends:
-        if all(copy is not other for other in waited):
-            copy.wait_send()
     for copy in done:
         copy.wait()
+    for copy in j_cp:
+        copy.wait_recv()
+    for copy in sends:
+        if all(copy is not other for other in a_cp):
+            copy.wait_send()
+
+
+def write_kernel(out, g_text, g_image, out_o, gt_o, gi_o):
+    out_o[...] = out[...]
+    gt_o[...] = g_text[...]
+    gi_o[...] = g_image[...]
+
+
+def grad_kernel(own, got, last_x, last_y, gate, up, *refs):
+    gg_o, gu_o = refs[-2:]
+    height, count = own.shape[0], 16
+
+    def rows_of(last):
+        for i in range(height // count):
+            at = pl.ds(i * count, count)
+            d = own[at, :].astype(jnp.float32) + got[at, :].astype(jnp.float32) + last[at, :].astype(jnp.float32)
+            gate_f, up_f, sig, act = silu_parts(gate[at, :], up[at, :])
+            gg_o[at, :] = (d * up_f * sig * (1.0 + gate_f * (1.0 - sig))).astype(jnp.bfloat16)
+            gu_o[at, :] = (d * act).astype(jnp.bfloat16)
+
+    @pl.when(pl.program_id(0) == 0)
+    def _():
+        rows_of(last_y)
+
+    @pl.when(pl.program_id(0) == 1)
+    def _():
+        rows_of(last_x)
+
+
+def grad_call(own, got, last_x, last_y, gate, up, skip, so_far):
+    ff, rows = own.shape
+    wide = 2 * LANES
+    steps = last_x.shape[1] // wide
+    tile = (ff // 2, wide)
+    every = pl.BlockSpec(tile, lambda a, j: (a, j + skip))
+    anywhere = pl.BlockSpec(memory_space=pl.ANY)
+    cells = 2 * last_x.shape[0] * last_x.shape[1]
+    block = jax.ShapeDtypeStruct((ff, rows), jnp.bfloat16)
+    return pl.pallas_call(
+        grad_kernel,
+        grid=(2, steps),
+        out_shape=(block, block),
+        in_specs=[
+            every,
+            every,
+            pl.BlockSpec(tile, lambda a, j: (0, a * j)),
+            pl.BlockSpec(tile, lambda a, j: (0, (1 - a) * j + a * (steps - 1))),
+            every,
+            every,
+        ]
+        + [anywhere] * len(so_far),
+        out_specs=(every, every),
+        input_output_aliases={6 + i: i for i in range(len(so_far))},
+        compiler_params=pltpu.CompilerParams(
+            dimension_semantics=("arbitrary", "arbitrary"), vmem_limit_bytes=VMEM_BYTES
+        ),
+        cost_estimate=pl.CostEstimate(flops=1000 * cells, bytes_accessed=14 * cells, transcendentals=cells),
+        name="gate_grads",
+    )(own, got, last_x, last_y, gate, up, *so_far)
 
 
 def square_per_device(
@@ -495,7 +542,11 @@
     block = shape((ff, rows), bf16)
     grad = shape((ff, 2 * feats), jnp.float32)
     anywhere = pl.BlockSpec(memory_space=pl.ANY)
-    outs = (shape((rows, feats), bf16), block, block, grad, grad)
+    aft = rows // (3 * LANES) * LANES
+    fore_part, aft_part = shape((ff // 2, rows - aft), bf16), shape((ff // 2, aft), bf16)
+    outs = (
+        shape((rows, feats), bf16), block, block, fore_part, aft_part, fore_part, aft_part, grad, grad,
+    )
     scratch = [
         pltpu.VMEM((4, ff, rows), bf16),
         pltpu.VMEM((4, ff, rows), bf16),
@@ -514,14 +565,13 @@
         pltpu.VMEM((4, q, feats), bf16),
         pltpu.VMEM((4, ff, rows), bf16),
         pltpu.VMEM((2, ff // 2, rows), bf16),
-        pltpu.VMEM((2, ff, rows), bf16),
         pltpu.VMEM((2, 2, ff // 2, 2 * LANES), jnp.float32),
         pltpu.SemaphoreType.DMA((64,)),
         pltpu.SemaphoreType.DMA((64,)),
         pltpu.SemaphoreType.DMA((32,)),
         pltpu.SemaphoreType.DMA((2, 2)),
     ]
-    ref_out, grad_gate, grad_up, g_text, g_image = pl.pallas_call(
+    out, own, got, early_x, late_x, early_y, late_y, g_text, g_image = pl.pallas_call(
         square_kernel,
         out_shape=outs,
         in_specs=[pl.BlockSpec(memory_space=pltpu.SMEM)] + [anywhere] * 13,
@@ -536,6 +586,35 @@
         pol_gate.T, pol_up.T, pol_modality.reshape(-1, LANES), pol_segment.reshape(-1, LANES), token_cotangent,
         pol_down_text.T, pol_down_image.T,
     )
+    across_x = [(i, i + 1 - 2 * (i % 2)) for i in range(n)]
+    across_y = [(i, (i + 2) % n) for i in range(n)]
+    early_x = lax.ppermute(early_x, "fsdp", across_x)
+    early_y = lax.ppermute(early_y, "fsdp", across_y)
+    late_x = lax.ppermute(late_x, "fsdp", across_x)
+    late_y = lax.ppermute(late_y, "fsdp", across_y)
+
+    wide = 2 * LANES
+    steps = 2 * feats // wide
+    out_spec = pl.BlockSpec((rows // (2 * steps), feats), lambda a, j: (a * steps + j, 0))
+    g_spec = pl.BlockSpec((ff // 2, wide), lambda a, j: (a, j))
+    ref_out, g_text, g_image = pl.pallas_call(
+        write_kernel,
+        grid=(2, steps),
+        out_shape=(shape((rows, feats), bf16), grad, grad),
+        in_specs=[out_spec, g_spec, g_spec],
+        out_specs=(out_spec, g_spec, g_spec),
+        compiler_params=pltpu.CompilerParams(
+            dimension_semantics=("arbitrary", "arbitrary"), vmem_limit_bytes=VMEM_BYTES
+        ),
+        cost_estimate=pl.CostEstimate(
+            flops=1000 * ff * feats, bytes_accessed=32 * ff * feats, transcendentals=0
+        ),
+        name="write_out",
+    )(out, g_text, g_image)
+
+    grads = grad_call(own, got, early_x, early_y, pol_gate.T, pol_up.T, 0, ())
+    skip = (rows - aft) // (2 * LANES)
+    grad_gate, grad_up = grad_call(own, got, late_x, late_y, pol_gate.T, pol_up.T, skip, grads)
     return (ref_out, grad_gate.T, grad_up.T, g_text.T, g_image.T)
 
 

time: 251 us -> 241 us (0.960)
  local copies, waits for them, and re-layouts: 13.3 us -> 0 us
  Pallas kernels: 236 us -> 229 us
  waiting for transfers between devices: 0 us -> 6.05 us
  starting transfers between devices: 0 us -> 4.12 us
    pallas_call x1, Pallas kernels: 236 us -> 209 us  [square_per_device(): pl.pallas_call(square_kernel, out_shape=outs, in_specs=[pl.BlockSpec(memo...]
    pallas_call x0 -> x3, Pallas kernels: none -> 19.9 us  [the longest x1 11 us: square_per_device(): pl.pallas_call(write_kernel, grid=(2, steps), out_shape=(shape((rows, fea...]
    unnamed x13 -> x0, local copies, waits for them, and re-layouts: 13.3 us -> none
    ppermute x0 -> x4, waiting for transfers between devices: none -> 6.05 us  [the longest x1 3.97 us: square_per_device(): early_x = lax.ppermute(early_x, 'fsdp', across_x)]
    ppermute x0 -> x4, starting transfers between devices: none -> 4.12 us  [the longest x1 1.44 us: square_per_device(): early_x = lax.ppermute(early_x, 'fsdp', across_x)]
  transfers between devices with their start and end apart: 0 -> 4, of which waited for: 0 -> 3; matrix products, arithmetic and copies ran while one was open for 0% -> 0% of each run, Pallas kernels for 0% -> 7%
where the time goes in v2:
time: 241 us; the launch traced here: 240 us
  Pallas kernels  229 us (95%)
  waiting for transfers between devices  6.05 us (3%)
  starting transfers between devices  4.12 us (2%)
    pallas_call x1, Pallas kernels, square_per_device(): pl.pallas_call(square_kernel, out_shape=outs, in_specs=[pl.BlockSpec(memo...  209 us
    pallas_call x1, Pallas kernels, square_per_device(): pl.pallas_call(write_kernel, grid=(2, steps), out_shape=(shape((rows, fea...  11 us
    pallas_call x2, Pallas kernels, grad_call(): pl.pallas_call(grad_kernel, grid=(2, steps), out_shape=(block, block), in...  8.97 us
  transfers between devices with their start and end apart: 4, of which 3 were waited for; matrix products, arithmetic and copies ran while one was open for 0% of the time, Pallas kernels for 7%

profile of v2, /device:TPU:28, one launch (start us, length us, event | category | flops | bytes accessed | tf_op | source)
XLA Modules:
  0.0 239.9 jit_solution(15819921523577698255)
XLA Ops:
  0.6 209.1 %square_step.1 = (bf16[768,512]{1,0:T(8,128)(2,1)}, bf16[1376,768]{1,0:T(8,128)(2,1)}, bf16[1376,768]{1,0:T(8,128)(2,1)}, bf16[688,512]{1,0:T(8,128)(2,1)}, bf16...) custom-call(f32[3]{0:T(128)} %margin.1, ...), custom_call_target="tpu_custom_call" | custom-call | tf_op jit(solution)/shard_map/square_step/pallas_call | solution.py:574
  209.8 1.4 collective-permute-start.2
  211.2 0.5 collective-permute-start.3
  211.7 1.0 collective-permute-start
  212.7 1.2 collective-permute-start.1
  213.9 11.0 %write_out.1 = (bf16[768,512]{1,0:T(8,128)(2,1)}, f32[1376,1024]{1,0:T(8,128)}, f32[1376,1024]{1,0:T(8,128)}) custom-call(bf16[768,512]{1,0:T(8,128)(2,1)} %get-tuple-element.21.out, f32[1376,1024]{1,0:T(8,128)} %get-tuple-element.22.g_text, f32[1376,1024]{1,0:T(8,128)} %get-tuple-element.23.g_image), custom_call_target="tpu_custom_call" | custom-call | flops 704512000 | bytes 22544384 | tf_op jit(solution)/shard_map/write_out/pallas_call | solution.py:600
  224.8 4.0 %collective-permute-done.2.last_x = bf16[688,512]{1,0:T(8,128)(2,1)} collective-permute-done((bf16[688,512]{1,0:T(8,128)(2,1)}, bf16[688,512]{1,0:T(8,128)(2,1)}, u32[]{:S(2)}, u32[]{:S(2)}) %collective-permute-start.2) | collective-permute-done | bytes 704544 | tf_op jit(solution)/shard_map/ppermute | solution.py:591
  228.8 1.4 collective-permute-done.3.last_y
  230.2 5.7 %gate_grads.2 = (bf16[1376,768]{1,0:T(8,128)(2,1)}, bf16[1376,768]{1,0:T(8,128)(2,1)}) custom-call(bf16[1376,768]{1,0:T(8,128)(2,1)} %get-tuple-element.25.own, bf16[1376,768]{1,0:T(8,128)(2,1)} %get-tuple-element.26.got, bf16[688,512]{1,0:T(8,128)(2,1)} %collective-permute-done.2.last_x, bf16[688,512]{1,0:T(8,128)(2,1)} %collective-permute-done.3.last_y, ...), custom_call_target="tpu_custom_call" | custom-call | flops 704512000 | bytes 9863168 | tf_op jit(solution)/shard_map/gate_grads/pallas_call | solution.py:495
  235.9 0.0 collective-permute-done.last_x
  235.9 0.7 collective-permute-done.1.last_y
  236.6 3.3 %gate_grads.3 = (bf16[1376,768]{1,0:T(8,128)(2,1)}, bf16[1376,768]{1,0:T(8,128)(2,1)}) custom-call(bf16[1376,768]{1,0:T(8,128)(2,1)} %get-tuple-element.25.own, bf16[1376,768]{1,0:T(8,128)(2,1)} %get-tuple-element.26.got, bf16[688,256]{1,0:T(8,128)(2,1)} %collective-permute-done.last_x, ...), custom_call_target="tpu_custom_call", output_to_operand_aliasing={{0}: (6, {}), {1}: (7, {})} | custom-call | flops 352256000 | bytes 4931584 | tf_op jit(solution)/shard_map/gate_grads/pallas_call | solution.py:495
Async XLA Ops:
  209.8 19.0 %collective-permute-start.2 = (bf16[688,512]{1,0:T(8,128)(2,1)}, bf16[688,512]{1,0:T(8,128)(2,1)}, u32[]{:S(2)}, u32[]{:S(2)}) collective-permute-start(bf16[688,512]{1,0:T(8,128)(2,1)} %get-tuple-element.29), channel_id=1, source_target_pairs={{0,8},{8,0},{16,24},{24,16},{1,9},{9,1},{17,25},{25,17},{2,10},{10... | collective-permute-start | bytes 2113544 | tf_op jit(solution)/shard_map/ppermute | solution.py:591
  211.2 19.0 %collective-permute-start.3 = (bf16[688,512]{1,0:T(8,128)(2,1)}, bf16[688,512]{1,0:T(8,128)(2,1)}, u32[]{:S(2)}, u32[]{:S(2)}) collective-permute-start(bf16[688,512]{1,0:T(8,128)(2,1)} %get-tuple-element.30), channel_id=1, source_target_pairs={{0,16},{8,24},{16,0},{24,8},{1,17},{9,25},{17,1},{25,9},{2,18},{10... | collective-permute-start | bytes 2113544 | tf_op jit(solution)/shard_map/ppermute | solution.py:592
  211.7 24.2 %collective-permute-start = (bf16[688,256]{1,0:T(8,128)(2,1)}, bf16[688,256]{1,0:T(8,128)(2,1)}, u32[]{:S(2)}, u32[]{:S(2)}) collective-permute-start(bf16[688,256]{1,0:T(8,128)(2,1)} %get-tuple-element.27), channel_id=1, source_target_pairs={{0,8},{8,0},{16,24},{24,16},{1,9},{9,1},{17,25},{25,17},{2,10},{10... | collective-permute-start | bytes 1056776 | tf_op jit(solution)/shard_map/ppermute | solution.py:593
  212.7 23.9 %collective-permute-start.1 = (bf16[688,256]{1,0:T(8,128)(2,1)}, bf16[688,256]{1,0:T(8,128)(2,1)}, u32[]{:S(2)}, u32[]{:S(2)}) collective-permute-start(bf16[688,256]{1,0:T(8,128)(2,1)} %get-tuple-element.28), channel_id=1, source_target_pairs={{0,16},{8,24},{16,0},{24,8},{1,17},{9,25},{17,1},{25,9},{2,18},{10... | collective-permute-start | bytes 1056776 | tf_op jit(solution)/shard_map/ppermute | solution.py:594

commit v3 on v2

--- a/solution.py
+++ b/solution.py
@@ -205,8 +205,6 @@
     ]
     small = [local(src, tags.at[i]) for i, src in enumerate((ref_mod, pol_mod, pol_seg))]
     small.append(local(cot_raw, own_cot))
-    w_ld = [local(ref_text, w.at[0]), local(ref_image, w.at[1])]
-    pol_ld = [local(pol_gate, dsend.at[2]), local(pol_up, dsend.at[3])]
 
     barrier = pltpu.get_barrier_semaphore()
     peers = [side[1], side[2], side[3]] + [up[r] for r in range(1, n)] + [sister]
@@ -226,6 +224,8 @@
         copy.wait()
     hidden_rows(0, 0, href)
     own_x = [remote(href.at[0, top], href.at[1, top], side[1])]
+    pol_ld = [local(pol_gate, dsend.at[2]), local(pol_up, dsend.at[3])]
+    w_ld = [local(ref_text, w.at[0]), local(ref_image, w.at[1])]
     for copy in loads[1]:
         copy.wait()
     hidden_rows(mid, 0, href)
@@ -483,11 +483,12 @@
         rows_of(last_x)
 
 
-def grad_call(own, got, last_x, last_y, gate, up, skip, so_far):
+def grad_call(own, got, last_x, last_y, gate, up, first, so_far):
     ff, rows = own.shape
-    wide = 2 * LANES
+    wide = min(last_x.shape[1], 4 * LANES)
     steps = last_x.shape[1] // wide
     tile = (ff // 2, wide)
+    skip = first // wide
     every = pl.BlockSpec(tile, lambda a, j: (a, j + skip))
     anywhere = pl.BlockSpec(memory_space=pl.ANY)
     cells = 2 * last_x.shape[0] * last_x.shape[1]
@@ -613,8 +614,7 @@
     )(out, g_text, g_image)
 
     grads = grad_call(own, got, early_x, early_y, pol_gate.T, pol_up.T, 0, ())
-    skip = (rows - aft) // (2 * LANES)
-    grad_gate, grad_up = grad_call(own, got, late_x, late_y, pol_gate.T, pol_up.T, skip, grads)
+    grad_gate, grad_up = grad_call(own, got, late_x, late_y, pol_gate.T, pol_up.T, rows - aft, grads)
     return (ref_out, grad_gate.T, grad_up.T, g_text.T, g_image.T)
 
 

time: 241 us -> 240 us (level)
  no operation moved by 1% of the time
where the time goes in v3:
time: 240 us
  Pallas kernels  228 us (95%)
  waiting for transfers between devices  6.82 us (3%)
  starting transfers between devices  4.12 us (2%)
    pallas_call x1, Pallas kernels, square_per_device(): pl.pallas_call(square_kernel, out_shape=outs, in_specs=[pl.BlockSpec(memo...  209 us
    pallas_call x1, Pallas kernels, square_per_device(): pl.pallas_call(write_kernel, grid=(2, steps), out_shape=(shape((rows, fea...  11 us
    pallas_call x2, Pallas kernels, grad_call(): pl.pallas_call(grad_kernel, grid=(2, steps), out_shape=(block, block), in...  8.22 us
  transfers between devices with their start and end apart: 4, of which 3 were waited for; matrix products, arithmetic and copies ran while one was open for 0% of the time, Pallas kernels for 7%

profile of v3, /device:TPU:28, one launch (start us, length us, event | category | flops | bytes accessed | tf_op | source)
XLA Modules:
  0.0 239.9 jit_solution(8325211968257179254)
XLA Ops:
  0.6 209.1 %square_step.1 = (bf16[768,512]{1,0:T(8,128)(2,1)}, bf16[1376,768]{1,0:T(8,128)(2,1)}, bf16[1376,768]{1,0:T(8,128)(2,1)}, bf16[688,512]{1,0:T(8,128)(2,1)}, bf16...) custom-call(f32[3]{0:T(128)} %margin.1, ...), custom_call_target="tpu_custom_call" | custom-call | tf_op jit(solution)/shard_map/square_step/pallas_call | solution.py:575
  209.8 1.5 collective-permute-start.2
  211.2 0.5 collective-permute-start.3
  211.7 1.0 collective-permute-start
  212.7 1.2 collective-permute-start.1
  213.9 11.0 %write_out.1 = (bf16[768,512]{1,0:T(8,128)(2,1)}, f32[1376,1024]{1,0:T(8,128)}, f32[1376,1024]{1,0:T(8,128)}) custom-call(bf16[768,512]{1,0:T(8,128)(2,1)} %get-tuple-element.21.out, f32[1376,1024]{1,0:T(8,128)} %get-tuple-element.22.g_text, f32[1376,1024]{1,0:T(8,128)} %get-tuple-element.23.g_image), custom_call_target="tpu_custom_call" | custom-call | flops 704512000 | bytes 22544384 | tf_op jit(solution)/shard_map/write_out/pallas_call | solution.py:601
  224.8 4.0 %collective-permute-done.2.last_x = bf16[688,512]{1,0:T(8,128)(2,1)} collective-permute-done((bf16[688,512]{1,0:T(8,128)(2,1)}, bf16[688,512]{1,0:T(8,128)(2,1)}, u32[]{:S(2)}, u32[]{:S(2)}) %collective-permute-start.2) | collective-permute-done | bytes 704544 | tf_op jit(solution)/shard_map/ppermute | solution.py:592
  228.8 1.4 collective-permute-done.3.last_y
  230.2 4.9 %gate_grads.2 = (bf16[1376,768]{1,0:T(8,128)(2,1)}, bf16[1376,768]{1,0:T(8,128)(2,1)}) custom-call(bf16[1376,768]{1,0:T(8,128)(2,1)} %get-tuple-element.25.own, bf16[1376,768]{1,0:T(8,128)(2,1)} %get-tuple-element.26.got, bf16[688,512]{1,0:T(8,128)(2,1)} %collective-permute-done.2.last_x, bf16[688,512]{1,0:T(8,128)(2,1)} %collective-permute-done.3.last_y, ...), custom_call_target="tpu_custom_call" | custom-call | flops 704512000 | bytes 9863168 | tf_op jit(solution)/shard_map/gate_grads/pallas_call | solution.py:496
  235.1 0.0 collective-permute-done.last_x
  235.2 1.5 collective-permute-done.1.last_y
  236.6 3.3 %gate_grads.3 = (bf16[1376,768]{1,0:T(8,128)(2,1)}, bf16[1376,768]{1,0:T(8,128)(2,1)}) custom-call(bf16[1376,768]{1,0:T(8,128)(2,1)} %get-tuple-element.25.own, bf16[1376,768]{1,0:T(8,128)(2,1)} %get-tuple-element.26.got, bf16[688,256]{1,0:T(8,128)(2,1)} %collective-permute-done.last_x, ...), custom_call_target="tpu_custom_call", output_to_operand_aliasing={{0}: (6, {}), {1}: (7, {})} | custom-call | flops 352256000 | bytes 4931584 | tf_op jit(solution)/shard_map/gate_grads/pallas_call | solution.py:496
Async XLA Ops:
  209.8 19.0 %collective-permute-start.2 = (bf16[688,512]{1,0:T(8,128)(2,1)}, bf16[688,512]{1,0:T(8,128)(2,1)}, u32[]{:S(2)}, u32[]{:S(2)}) collective-permute-start(bf16[688,512]{1,0:T(8,128)(2,1)} %get-tuple-element.29), channel_id=1, source_target_pairs={{0,8},{8,0},{16,24},{24,16},{1,9},{9,1},{17,25},{25,17},{2,10},{10... | collective-permute-start | bytes 2113544 | tf_op jit(solution)/shard_map/ppermute | solution.py:592
  211.2 19.0 %collective-permute-start.3 = (bf16[688,512]{1,0:T(8,128)(2,1)}, bf16[688,512]{1,0:T(8,128)(2,1)}, u32[]{:S(2)}, u32[]{:S(2)}) collective-permute-start(bf16[688,512]{1,0:T(8,128)(2,1)} %get-tuple-element.30), channel_id=1, source_target_pairs={{0,16},{8,24},{16,0},{24,8},{1,17},{9,25},{17,1},{25,9},{2,18},{10... | collective-permute-start | bytes 2113544 | tf_op jit(solution)/shard_map/ppermute | solution.py:593
  211.7 23.4 %collective-permute-start = (bf16[688,256]{1,0:T(8,128)(2,1)}, bf16[688,256]{1,0:T(8,128)(2,1)}, u32[]{:S(2)}, u32[]{:S(2)}) collective-permute-start(bf16[688,256]{1,0:T(8,128)(2,1)} %get-tuple-element.27), channel_id=1, source_target_pairs={{0,8},{8,0},{16,24},{24,16},{1,9},{9,1},{17,25},{25,17},{2,10},{10... | collective-permute-start | bytes 1056776 | tf_op jit(solution)/shard_map/ppermute | solution.py:594
  212.7 23.9 %collective-permute-start.1 = (bf16[688,256]{1,0:T(8,128)(2,1)}, bf16[688,256]{1,0:T(8,128)(2,1)}, u32[]{:S(2)}, u32[]{:S(2)}) collective-permute-start(bf16[688,256]{1,0:T(8,128)(2,1)} %get-tuple-element.28), channel_id=1, source_target_pairs={{0,16},{8,24},{16,0},{24,8},{1,17},{9,25},{17,1},{25,9},{2,18},{10... | collective-permute-start | bytes 1056776 | tf_op jit(solution)/shard_map/ppermute | solution.py:595
